TPU v7x, 256 devices: a whole 4x4x8 slice. The times are simulated.
256 devices in a mesh: tower: 2 (over x_lo), blk: 128 (over z, y, x_hi, core).
Axes of the slice: x: 4 (x_hi: 2, x_lo: 2; x = x_hi * 2 + x_lo), y: 4, z: 8, core: 2. Of those that a mesh axis runs over, the one named last changes fastest.
Arguments:
- pooled: bfloat16 [2, 16384, 1152], P('tower', 'blk'), may hold values from -6 to 6
- final_gain: float32 [2, 1152], P('tower'), may hold values from 0.5 to 1.5
- head_weight: bfloat16 [2, 1152, 1152], P('tower'), may hold values from -0.1875 to 0.1875
- pair_ids: int32 [16384], replicated, may hold values from 0 to 16383
- log_scale: float32 [1], replicated, may hold values from 4.2 to 4.7
- bias: float32 [1], replicated, may hold values from -4 to -1
Outputs:
- emb_grad: float32 [2, 16384, 1152], P('tower', 'blk')
Inputs may be any that keep to these rules, and one draw needn't show every extreme that they name: `pair_ids`: examples with equal ids form positive pairs; every example is a positive pair with its own image and text.
All inputs are finite; a program needn't handle non-finite values.
Results may differ from a plain program's by a relative error of at most 0.0043.
Values may be sent and summed in bfloat16 or wider, within the bound.
No kernel may reach another device: no remote copies, remote signals or barrier semaphores. Data moves between devices by JAX's collectives and lax.ppermute only.
A program may use at most 192 MiB of HBM per device.

v0:
```python
import jax
import jax.numpy as jnp
from jax import lax
from jax.sharding import PartitionSpec as P


def partner(value, axis, stride):
    mask = 2**stride
    pairs = [(source, source ^ mask) for source in range(lax.axis_size(axis))]
    return lax.ppermute(value, axis, pairs)


def embed_rows(feats, gain, weight):
    values = feats.astype(jnp.float32)
    center = values - jnp.mean(values, axis=-1, keepdims=True)
    spread = jnp.mean(center * center, axis=-1, keepdims=True)
    normed = (center * lax.rsqrt(spread + 1e-06) * gain).astype(jnp.bfloat16)
    head = jnp.dot(normed, weight, preferred_element_type=jnp.float32)
    length = jnp.sum(head * head, axis=-1, keepdims=True)
    return (head * lax.rsqrt(length + 1e-06)).astype(jnp.bfloat16)


def pair_coef(fixed_rows, moving_rows, fixed_ids, moving_ids, scale, shift):
    logits = (
        scale
        * lax.dot_general(
            fixed_rows, moving_rows, (((1,), (1,)), ((), ())), preferred_element_type=jnp.float32
        )
        + shift
    )
    sign = jnp.where(fixed_ids[:, None] == moving_ids[None, :], jnp.float32(1.0), jnp.float32(-1.0))
    return (-sign * jax.nn.sigmoid(-sign * logits)).astype(jnp.bfloat16)


def pair_forces(fixed_rows, moving_rows, fixed_ids, moving_ids, scale, shift):
    coef = pair_coef(fixed_rows, moving_rows, fixed_ids, moving_ids, scale, shift)
    return jnp.dot(coef, moving_rows, preferred_element_type=jnp.float32)


def on_device(pooled, final_gain, head_weight, pair_ids, log_scale, bias):
    local_embed = embed_rows(pooled[0], final_gain[0], head_weight[0])
    count = local_embed.shape[0]
    scale = jnp.exp(log_scale[0])
    shift = bias[0]
    block_index = lax.axis_index("blk")
    local_ids = lax.dynamic_slice_in_dim(pair_ids, block_index * count, count)
    partner_embed = partner(local_embed, "tower", 0)
    total = pair_forces(
        local_embed,
        lax.all_gather(partner_embed, "blk", axis=0, tiled=True),
        local_ids,
        pair_ids,
        scale,
        shift,
    )
    return total[None]


def solution(mesh):
    placed = (P("tower", "blk", None), P("tower", None), P("tower", None, None), P(), P(), P())
    return jax.shard_map(
        on_device, mesh=mesh, in_specs=placed, out_specs=P("tower", "blk", None), check_vma=False
    )
```

profile of v0, /device:TPU:1, one launch (start us, length us, event | category | flops | bytes accessed | tf_op | source)
XLA Modules:
  0.0 296.5 jit_solution(8610071853615321268)
XLA Ops:
  6.5 0.0 copy-start
  6.5 0.0 all-gather.2.cloned.1.call-start
  6.5 1.2 convert_reduce_fusion
  7.8 1.2 fusion.23
  9.0 0.7 reduce.1
  9.7 0.0 copy-done
  9.7 1.7 multiply_reduce_fusion
  11.4 0.1 multiply_convert_fusion
  11.5 2.1 collective-permute-start
  13.7 5.5 %collective-permute-done = bf16[128,1152]{1,0:T(8,128)(2,1)S(1)} collective-permute-done((bf16[128,1152]{1,0:T(8,128)(2,1)S(1)}, bf16[128,1152]{1,0:T(8,128)(2,1)S(1)}, u32[]{:S(2)}, u32[]{:S(2)}) %collective-permute-start) | collective-permute-done | bytes 294944 | tf_op jit(solution)/shard_map/ppermute | solution.py:10
  19.1 0.0 copy-start.1
  19.1 0.7 copy-done.1
  19.8 0.0 all-gather.2.cloned.1.call-update
  21.2 0.8 dynamic_slice.3
  22.0 231.2 %all-gather.2.cloned.1.call-done = bf16[16384,1152]{1,0:T(8,128)(2,1)} async-done(((bf16[128,1152]{1,0:T(8,128)(2,1)}), bf16[16384,1152]{1,0:T(8,128)(2,1)}) %all-gather.2.cloned.1.call-update) | async-done | bytes 37748752 | tf_op jit(solution)/shard_map/all_gather | solution.py:50
  253.2 36.4 %fusion.17 = f32[1,128,1152]{2,1,0:T(8,128)} fusion(bf16[16384,1152]{1,0:T(8,128)(2,1)} %all-gather.2.cloned.1.call-done, bf16[128,1152]{1,0:T(8,128)(2,1)S(1)} %multiply_convert_fusion, f32[]{:T(128)} %bitcast.25, f32[]{:T(128)} %bitcast, s32[16384]{0:T(1024)} %param.9, s32[128]{0:T(128)S(1)} %dynamic_slice.3), kind=kOutput, calls=%fused_computation.18 | convolution fusion | flops 9686745088 | bytes 38699528 | tf_op jit(solution)/shard_map/dot_general | solution.py:37
  (3 shorter events, 0.0 us)
Async XLA Ops:
  6.5 3.2 %copy-start = (bf16[1,1152,1152]{2,1,0:T(8,128)(2,1)S(1)}, bf16[1,1152,1152]{2,1,0:T(8,128)(2,1)}, u32[]{:S(2)}) copy-start(bf16[1,1152,1152]{2,1,0:T(8,128)(2,1)} %param.8) | copy-start | bytes 7962628
  6.5 246.7 %all-gather.2.cloned.1.call-start = ((), (), s32[]{:S(2)}) async-start(), calls=%async_computation | async-start | bytes 38043648 | tf_op jit(solution)/shard_map/all_gather | solution.py:50
  11.5 7.6 %collective-permute-start = (bf16[128,1152]{1,0:T(8,128)(2,1)S(1)}, bf16[128,1152]{1,0:T(8,128)(2,1)S(1)}, u32[]{:S(2)}, u32[]{:S(2)}) collective-permute-start(bf16[128,1152]{1,0:T(8,128)(2,1)S(1)} %multiply_convert_fusion), channel_id=1, source_target_pairs={{0,128},{128,0},{1,129},{129,1},{2,130},{130,2},{3,131},{131,3},{4... | collective-permute-start | bytes 884744 | tf_op jit(solution)/shard_map/ppermute | solution.py:10
  19.1 0.7 copy-start.1
Sparse Core Ops, SparseCore 0:
  20.0 233.1 all-gather.1
where the time goes:
time: 297 us; the launch traced here: 296 us
  waiting for transfers between devices  237 us (80%)
  matrix products  38.1 us (13%)
  between operations  14.8 us (5%)
  other arithmetic  3.27 us (1%)
    all_gather x1, waiting for transfers between devices, on_device(): lax.all_gather(partner_embed, 'blk', axis=0, tiled=True)  231 us
    dot_general x1, matrix products, pair_forces(): return jnp.dot(coef, moving_rows, preferred_element_type=jnp.float32)  36.4 us
  transfers between devices with their start and end apart: 2, of which 2 were waited for; matrix products, arithmetic and copies ran while one was open for 0% of the time, Pallas kernels for 0%

commit v1 on v0

--- a/solution.py
+++ b/solution.py
@@ -2,6 +2,11 @@
 import jax.numpy as jnp
 from jax import lax
 from jax.sharding import PartitionSpec as P
+
+
+def gather_over(x, mesh_axis, along):
+    sent = jnp.stack([x] * lax.axis_size(mesh_axis))
+    return jnp.concatenate(lax.all_to_all(sent, mesh_axis, 0, 0), axis=along)
 
 
 def partner(value, axis, stride):
@@ -46,12 +51,7 @@
     local_ids = lax.dynamic_slice_in_dim(pair_ids, block_index * count, count)
     partner_embed = partner(local_embed, "tower", 0)
     total = pair_forces(
-        local_embed,
-        lax.all_gather(partner_embed, "blk", axis=0, tiled=True),
-        local_ids,
-        pair_ids,
-        scale,
-        shift,
+        local_embed, gather_over(partner_embed, "blk", 0), local_ids, pair_ids, scale, shift
     )
     return total[None]
 

time: 297 us -> 939 us (3.16)
  waiting for transfers between devices: 237 us -> 856 us
  starting transfers between devices: 2.12 us -> 20.3 us
  between operations: 14.8 us -> 1.39 us
  local copies, waits for them, and re-layouts: 1.48 us -> 12.9 us
    all_to_all x0 -> x1, waiting for transfers between devices: none -> 850 us  [gather_over(): return jnp.concatenate(lax.all_to_all(sent, mesh_axis, 0, 0), axis=along)]
    all_gather x1 -> x0, waiting for transfers between devices: 231 us -> none  [on_device(): lax.all_gather(partner_embed, 'blk', axis=0, tiled=True)]
    all_to_all x0 -> x1, starting transfers between devices: none -> 18.2 us  [gather_over(): return jnp.concatenate(lax.all_to_all(sent, mesh_axis, 0, 0), axis=along)]
    another operation x0 -> x1, local copies, waits for them, and re-layouts: none -> 12.8 us  [gather_over(): sent = jnp.stack([x] * lax.axis_size(mesh_axis))]
where the time goes in v1:
time: 939 us; the launch traced here: 932 us
  waiting for transfers between devices  856 us (91%)
  matrix products  38.1 us (4%)
  starting transfers between devices  20.3 us (2%)
  local copies, waits for them, and re-layouts  12.9 us (1%)
    all_to_all x1, waiting for transfers between devices, gather_over(): return jnp.concatenate(lax.all_to_all(sent, mesh_axis, 0, 0), axis=along)  850 us
    dot_general x1, matrix products, pair_forces(): return jnp.dot(coef, moving_rows, preferred_element_type=jnp.float32)  36.4 us
  transfers between devices with their start and end apart: 2, of which 2 were waited for; matrix products, arithmetic and copies ran while one was open for 0% of the time, Pallas kernels for 0%

profile of v1, /device:TPU:1, one launch (start us, length us, event | category | flops | bytes accessed | tf_op | source)
XLA Modules:
  0.0 931.8 jit_solution(15062305598932261297)
XLA Ops:
  0.0 0.0 copy-start
  0.0 1.2 convert_reduce_fusion
  1.2 1.2 fusion.23
  2.4 0.7 reduce.1
  3.2 0.0 copy-done
  3.2 1.7 multiply_reduce_fusion
  4.9 0.1 multiply_convert_fusion
  5.0 2.1 collective-permute-start
  7.1 5.5 collective-permute-done
  12.6 12.8 %stack.2 = bf16[128,128,1152]{2,1,0:T(8,128)(2,1)} broadcast(bf16[128,1152]{1,0:T(8,128)(2,1)S(1)} %collective-permute-done), dimensions={1,2} | broadcast | bytes 38043648 | tf_op jit(solution)/shard_map/stack | solution.py:8
  25.4 0.0 copy-start.2
  25.4 18.2 %all-to-all-start = ((bf16[128,128,1152]{2,1,0:T(8,128)(2,1)}), bf16[128,128,1152]{2,1,0:T(8,128)(2,1)}, u32[]{:S(2)}, u32[]{:S(2)}) async-start(bf16[128,128,1152]{2,1,0:T(8,128)(2,1)} %stack.2), calls=%async_computation | async-start | bytes 75497472 | tf_op jit(solution)/shard_map/all_to_all | solution.py:9
  44.9 0.0 copy-done.2
  44.9 0.1 dynamic_slice.3
  45.0 850.4 %all-to-all-done = bf16[128,128,1152]{2,1,0:T(8,128)(2,1)} async-done(((bf16[128,128,1152]{2,1,0:T(8,128)(2,1)}), bf16[128,128,1152]{2,1,0:T(8,128)(2,1)}, u32[]{:S(2)}, u32[]{:S(2)}) %all-to-all-start) | async-done | bytes 37748768 | tf_op jit(solution)/shard_map/all_to_all | solution.py:9
  895.4 0.0 copy-start.1
  895.4 36.4 %fusion.17 = f32[1,128,1152]{2,1,0:T(8,128)} fusion(bf16[16384,1152]{1,0:T(8,128)(2,1)} %bitcast.4, bf16[128,1152]{1,0:T(8,128)(2,1)S(1)} %multiply_convert_fusion, f32[]{:T(128)} %bitcast.26, f32[]{:T(128)} %bitcast, s32[16384]{0:T(1024)S(1)} %copy-done.2, s32[128]{0:T(128)S(1)} %dynamic_slice.3), kind=kOutput, calls=%fused_computation.18 | convolution fusion | flops 9686745088 | bytes 38699528 | tf_op jit(solution)/shard_map/dot_general | solution.py:42
  931.8 0.0 copy-done.1
  (3 shorter events, 0.0 us)
Async XLA Ops:
  0.0 3.2 copy-start
  5.0 7.6 collective-permute-start
  25.4 19.5 %copy-start.2 = (s32[16384]{0:T(1024)S(1)}, s32[16384]{0:T(1024)}, u32[]{:S(2)}) copy-start(s32[16384]{0:T(1024)} %param.9) | copy-start | bytes 196612
  25.4 870.0 %all-to-all-start = ((bf16[128,128,1152]{2,1,0:T(8,128)(2,1)}), bf16[128,128,1152]{2,1,0:T(8,128)(2,1)}, u32[]{:S(2)}, u32[]{:S(2)}) async-start(bf16[128,128,1152]{2,1,0:T(8,128)(2,1)} %stack.2), calls=%async_computation | async-start | bytes 75497472 | tf_op jit(solution)/shard_map/all_to_all | solution.py:9
  895.4 36.4 %copy-start.1 = (bf16[1,1152,1152]{2,1,0:T(8,128)(2,1)S(1)}, bf16[1,1152,1152]{2,1,0:T(8,128)(2,1)}, u32[]{:S(2)}) copy-start(bf16[1,1152,1152]{2,1,0:T(8,128)(2,1)} %param.8) | copy-start | bytes 7962628
